TPU v7x, 32 devices: a whole 2x2x4 slice. The times are simulated.
32 devices in a mesh: patch: 16 (over z, y, x), batch: 2 (over core).
Axes of the slice: x: 2, y: 2, z: 4, core: 2. Of those that a mesh axis runs over, the one named last changes fastest.
Arguments:
- tokens: bfloat16 [4096, 1152], P(('batch', 'patch')), parts along dimension 0, may hold values from -6 to 6
- slots: int32 [4096], P(('batch', 'patch')), parts along dimension 0, may hold values from 0 to 127, as said below
- counts: int32 [32], P(('batch', 'patch')), parts along dimension 0, may hold values from 32 to 128, as said below
- shift: float32 [1152], replicated, may hold values from -3 to 3
- scale: float32 [1152], replicated, may hold values from -3 to 3
- gate: float32 [1152], replicated, may hold values from -4 to 4
- w_qkv: bfloat16 [1152, 3456], replicated, may hold values from -1 to 1
- w_out: bfloat16 [1152, 1152], replicated, may hold values from -0.1875 to 0.1875
Outputs:
- result: bfloat16 [4096, 1152], P(('batch', 'patch')), parts along dimension 0
There are 2 independent parts, one for each index of `batch`. A program takes and returns all parts, laid end to end along the dimension named above; an argument that names none is the same for every part. Nothing has to cross between parts.
Inputs may be any that keep to these rules, and one draw needn't show every extreme that they name: `counts`: at least a quarter of each block's slots are live. The live slots of all blocks of an image number exactly 80 times the number of patch devices, and all blocks of some device are full. `slots`: every token's slot is below its block's count, and every slot below the count holds at least one token.
All inputs are finite; a program needn't handle non-finite values.
Results may differ from a plain program's by a relative error of at most 0.011.
Values may be sent and summed in bfloat16 or wider, within the bound.
A program may use at most 192 MiB of HBM per device.

v0:
```python
import jax
import jax.numpy as jnp
from jax import lax
from jax.sharding import PartitionSpec as P

HEADS = 16
BLK = 128


def layer_norm(merged, shift, scale):
    values = merged.astype(jnp.float32)
    center = jnp.mean(values, axis=-1, keepdims=True)
    spread = jnp.mean((values - center) ** 2, axis=-1, keepdims=True)
    return ((values - center) * lax.rsqrt(spread + 1e-06) * (1.0 + scale) + shift).astype(
        jnp.bfloat16
    )


def size_bias(sizes):
    return jnp.log(jnp.maximum(sizes.astype(jnp.float32), 1.0))


def empty_carry(heads, query_rows, head_size):
    return (
        jnp.full((heads, query_rows), -1e30, jnp.float32),
        jnp.zeros((heads, query_rows), jnp.float32),
        jnp.zeros((heads, query_rows, head_size), jnp.float32),
    )


def finish(accum, total):
    heads, query_rows, head_size = accum.shape
    return (
        (accum / total[:, :, None])
        .transpose(1, 0, 2)
        .reshape(query_rows, heads * head_size)
        .astype(jnp.bfloat16)
    )


def attend_piece(query, carry, keys, values, bias, inverse):
    top, total, accum = carry
    key_rows = keys.shape[0]
    heads = query.shape[1]
    key_heads = keys.reshape(key_rows, heads, -1)
    value_heads = values.reshape(key_rows, heads, -1)
    score = (
        jnp.einsum("qhe,khe->hqk", query, key_heads, preferred_element_type=jnp.float32) * inverse
        + bias[None, None, :]
    )
    new_top = jnp.maximum(top, jnp.max(score, axis=-1))
    probs = jnp.exp(score - new_top[:, :, None])
    total = jnp.sum(probs, axis=-1)
    update = jnp.einsum(
        "hqk,khe->hqe", probs.astype(jnp.bfloat16), value_heads, preferred_element_type=jnp.float32
    )
    return (new_top, total, update)


def body(tokens, slots, counts, shift, scale, gate, w_qkv, w_out):
    rows, width = tokens.shape
    nblk = rows // BLK
    heads = HEADS
    head_size = width // heads
    inverse = 1.0 / head_size**0.5
    onehot = slots.reshape(nblk, BLK)[:, :, None] == jnp.arange(BLK, dtype=jnp.int32)[None, None, :]
    sums = jnp.einsum(
        "bts,btd->bsd",
        onehot.astype(jnp.bfloat16),
        tokens.reshape(nblk, BLK, width),
        preferred_element_type=jnp.float32,
    )
    members = jnp.sum(onehot.astype(jnp.float32), axis=1)
    merged = (
        (sums / jnp.maximum(members, 1.0)[:, :, None]).astype(jnp.bfloat16).reshape(rows, width)
    )
    normed = layer_norm(merged, shift, scale)
    sizes = members.reshape(rows).astype(jnp.bfloat16)
    qkv = jnp.dot(normed, w_qkv, preferred_element_type=jnp.float32)
    query = qkv[:, :width].astype(jnp.bfloat16)
    keys = qkv[:, width : 2 * width].astype(jnp.bfloat16)
    values = qkv[:, 2 * width :].astype(jnp.bfloat16)
    alive = (
        (jnp.arange(BLK, dtype=jnp.int32)[None, :] < counts[:, None])
        .reshape(rows)
        .astype(jnp.bfloat16)
    )
    query_heads = query.reshape(rows, heads, head_size)
    keys_part = lax.all_gather(keys, "patch", axis=0, tiled=True)
    values_part = lax.all_gather(values, "patch", axis=0, tiled=True)
    sizes_part = lax.all_gather(sizes, "patch", axis=0, tiled=True)
    alive_part = lax.all_gather(alive, "patch", axis=0, tiled=True)
    bias = jnp.where(alive_part > 0, size_bias(sizes_part), -1e30)
    top, total, accum = attend_piece(
        query_heads, empty_carry(heads, rows, head_size), keys_part, values_part, bias, inverse
    )
    attended = finish(accum, total)
    projected = jnp.dot(attended, w_out, preferred_element_type=jnp.float32)
    branch = jnp.einsum(
        "bts,bsd->btd",
        onehot.astype(jnp.float32),
        projected.reshape(nblk, BLK, width),
        precision=lax.Precision.HIGHEST,
    ).reshape(rows, width)
    return (tokens.astype(jnp.float32) + gate * branch).astype(jnp.bfloat16)


def solution(mesh):
    return jax.shard_map(
        body,
        mesh=mesh,
        in_specs=(
            P(("batch", "patch"), None),
            P(("batch", "patch")),
            P(("batch", "patch")),
            P(),
            P(),
            P(),
            P(),
            P(),
        ),
        out_specs=P(("batch", "patch"), None),
        check_vma=False,
    )
```

profile of v0, /device:TPU:0, one launch (start us, length us, event | category | flops | bytes accessed | tf_op | source)
XLA Modules:
  0.0 205.7 jit_solution(10820672473933980348)
XLA Ops:
  6.5 0.0 copy-start
  6.5 0.0 all-gather.5.cloned.1.call-start
  6.5 0.9 convert_reduce_fusion
  7.5 1.4 fusion.27
  8.9 0.2 multiply_reduce_fusion
  9.1 0.7 broadcast_add_fusion
  9.8 4.7 %convolution_convert_fusion = bf16[128,3456]{1,0:T(8,128)(2,1)S(1)} fusion(bf16[1152,3456]{1,0:T(8,128)(2,1)} %param.14, f32[128,1152]{1,0:T(8,128)S(1)} %get-tuple-element.11, f32[1152]{0:T(1024)} %param.11, f32[1152]{0:T(1024)S(1)} %broadcast_add_fusion, f32[128]{0:T(128)S(1)} %add_rsqrt_fusion, f32[128]{0:T(128)S(1)} %broadcast_multiply_fusion), kind=kOutput, calls=%fused_computation.6 | convolution fusion | flops 1020395520 | bytes 9447424 | tf_op jit(solution)/shard_map/dot_general | solution.py:79
  14.5 0.9 fusion.26
  15.4 0.0 all-gather.5.cloned.1.call-update
  15.4 0.0 all-gather.7.cloned.1.call-start
  15.5 0.7 all-gather.7.cloned.1.call-update
  16.2 0.2 copy.18
  17.1 42.7 %all-gather.1 = bf16[16,1,128]{2,1,0:T(2,128)(2,1)S(1)} all-gather(bf16[1,1,128]{2,1,0:T(2,128)(2,1)S(1)} %get-tuple-element.8), channel_id=1, replica_groups=mesh['patch'=16,'batch'=2] {'patch'}, dimensions={0}, use_global_device_ids=true | all-gather | bytes 4352 | tf_op jit(solution)/shard_map/all_gather | solution.py:91
  59.7 36.4 %all-gather = bf16[16,1,128]{2,1,0:T(2,128)(2,1)S(1)} all-gather(bf16[1,1,128]{2,1,0:T(2,128)(2,1)S(1)} %fusion.24), channel_id=1, replica_groups=mesh['patch'=16,'batch'=2] {'patch'}, dimensions={0}, use_global_device_ids=true | all-gather | bytes 4352 | tf_op jit(solution)/shard_map/all_gather | solution.py:92
  96.1 2.0 all-gather.5.cloned.1.call-done
  98.1 6.7 %copy.19 = bf16[2048,1152]{0,1:T(8,128)(2,1)} copy(bf16[2048,1152]{1,0:T(8,128)(2,1)} %all-gather.5.cloned.1.call-done) | data formatting | bytes 9437184 | tf_op jit(solution)/shard_map/all_gather | solution.py:89
  104.9 4.5 %fusion = (f32[16,128]{1,0:T(8,128)S(1)}, f32[16,128,2048]{2,1,0:T(8,128)S(1)}) fusion(f32[2048]{0:T(1024)S(1)} %bitcast.30, bf16[128,16,72]{0,2,1:T(8,128)(2,1)S(1)} %bitcast.28, bf16[2048,16,72]{0,2,1:T(8,128)(2,1)} %bitcast.26), kind=kOutput, calls=%fused_computation.2 | convolution fusion | flops 616560640 | bytes 21807104 | tf_op jit(solution)/shard_map/qhe,khe->hqk/dot_general | solution.py:48
  109.3 0.0 copy-start.1
  109.4 5.7 %copy-done.1 = f32[16,128,2048]{2,1,0:T(8,128)} copy-done((f32[16,128,2048]{2,1,0:T(8,128)}, f32[16,128,2048]{2,1,0:T(8,128)S(1)}, u32[]{:S(2)}) %copy-start.1) | copy-done | bytes 16777240
  115.1 3.8 %fusion.1 = f32[16,128]{1,0:T(8,128)S(1)} fusion(f32[16,128,2048]{2,1,0:T(8,128)S(1)} %get-tuple-element.13, f32[16,128]{1,0:T(8,128)S(1)} %broadcast_maximum_fusion, f32[2048]{0:T(1024)S(1)} %bitcast.31), kind=kLoop, calls=%fused_computation.3 | loop fusion | flops 16775168 | bytes 16801792 | tf_op jit(solution)/shard_map/reduce_sum | solution.py:53
  118.8 60.6 %all-gather.7.cloned.1.call-done = bf16[2048,1152]{1,0:T(8,128)(2,1)} async-done(((bf16[128,1152]{1,0:T(8,128)(2,1)}), bf16[2048,1152]{1,0:T(8,128)(2,1)}) %all-gather.7.cloned.1.call-update) | async-done | bytes 4718608 | tf_op jit(solution)/shard_map/all_gather | solution.py:90
  179.4 6.7 %copy.20 = bf16[2048,1152]{0,1:T(8,128)(2,1)} copy(bf16[2048,1152]{1,0:T(8,128)(2,1)} %all-gather.7.cloned.1.call-done) | data formatting | bytes 9437184 | tf_op jit(solution)/shard_map/all_gather | solution.py:90
  186.1 0.0 copy-start.2
  186.1 0.0 copy-start.3
  186.1 0.0 copy-start.4
  186.1 10.9 %fusion.15 = bf16[128,16,72]{0,2,1:T(8,128)(2,1)S(1)} fusion(bf16[2048,16,72]{0,2,1:T(8,128)(2,1)} %bitcast.27, f32[16,128,2048]{2,1,0:T(8,128)} %copy-done.1, f32[16,128]{1,0:T(8,128)S(1)} %broadcast_maximum_fusion, f32[2048]{0:T(1024)S(1)} %bitcast.32, f32[128,16]{0,1:T(8,128)S(1)} %bitcast.33), kind=kOutput, calls=%fused_computation.15 | convolution fusion | flops 621051904 | bytes 21815296 | tf_op jit(solution)/shard_map/hqk,khe->hqe/dot_general | solution.py:54
  197.0 0.0 copy-done
  197.0 0.6 fusion.28
  197.6 0.0 copy-done.2
  197.6 0.0 copy-done.3
  197.7 0.0 copy-done.4
  197.7 1.2 fusion.8
  (6 shorter events, 0.1 us)
Async XLA Ops:
  6.5 190.5 %copy-start = (bf16[1152,1152]{1,0:T(8,128)(2,1)S(1)}, bf16[1152,1152]{1,0:T(8,128)(2,1)}, u32[]{:S(2)}) copy-start(bf16[1152,1152]{1,0:T(8,128)(2,1)} %param.15) | copy-start | bytes 7962628
  6.5 91.6 %all-gather.5.cloned.1.call-start = ((), (), s32[]{:S(2)}) async-start(), calls=%async_computation | async-start | bytes 5013504 | tf_op jit(solution)/shard_map/all_gather | solution.py:89
  15.4 163.9 %all-gather.7.cloned.1.call-start = ((), (), s32[]{:S(2)}) async-start(), calls=%async_computation.1 | async-start | bytes 5013504 | tf_op jit(solution)/shard_map/all_gather | solution.py:90
  109.3 5.7 %copy-start.1 = (f32[16,128,2048]{2,1,0:T(8,128)}, f32[16,128,2048]{2,1,0:T(8,128)S(1)}, u32[]{:S(2)}) copy-start(f32[16,128,2048]{2,1,0:T(8,128)S(1)} %get-tuple-element.13) | copy-start | bytes 50331652
  186.1 11.5 %copy-start.2 = (bf16[128,1152]{1,0:T(8,128)(2,1)S(1)}, bf16[128,1152]{1,0:T(8,128)(2,1)}, u32[]{:S(2)}) copy-start(bf16[128,1152]{1,0:T(8,128)(2,1)} %param.8) | copy-start | bytes 884740
  186.1 11.5 %copy-start.3 = (f32[1152]{0:T(1024)S(1)}, f32[1152]{0:T(1024)}, u32[]{:S(2)}) copy-start(f32[1152]{0:T(1024)} %param.13) | copy-start | bytes 13828
  186.1 11.5 %copy-start.4 = (s32[128]{0:T(128)S(1)}, s32[128]{0:T(128)}, u32[]{:S(2)}) copy-start(s32[128]{0:T(128)} %param.9) | copy-start | bytes 1540
Sparse Core Ops, SparseCore 0:
  15.6 82.5 all-gather.4
  100.9 78.4 all-gather.6
where the time goes:
time: 206 us
  blocking collectives  79 us (38%)
  waiting for transfers between devices  63.3 us (31%)
  matrix products  23.3 us (11%)
  local copies, waits for them, and re-layouts  20.3 us (10%)
  between operations  14.2 us (7%)
  other arithmetic  5.63 us (3%)
    all_gather x1, waiting for transfers between devices, body(): values_part = lax.all_gather(values, 'patch', axis=0, tiled=True)  60.6 us
    all_gather x1, blocking collectives, body(): sizes_part = lax.all_gather(sizes, 'patch', axis=0, tiled=True)  42.7 us
    all_gather x1, blocking collectives, body(): alive_part = lax.all_gather(alive, 'patch', axis=0, tiled=True)  36.4 us
    dot_general x1, matrix products, attend_piece(): jnp.einsum('hqk,khe->hqe', probs.astype(jnp.bfloat16), value_heads, prefe...  10.9 us
    all_gather x1, local copies, waits for them, and re-layouts, body(): values_part = lax.all_gather(values, 'patch', axis=0, tiled=True)  6.74 us
    all_gather x1, local copies, waits for them, and re-layouts, body(): keys_part = lax.all_gather(keys, 'patch', axis=0, tiled=True)  6.74 us
    unnamed x10, local copies, waits for them, and re-layouts  5.71 us
    dot_general x1, matrix products, body(): qkv = jnp.dot(normed, w_qkv, preferred_element_type=jnp.float32)  4.71 us
  transfers between devices with their start and end apart: 2, of which 2 were waited for; matrix products, arithmetic and copies ran while one was open for 7% of the time, Pallas kernels for 0%

commit v1 on v0

--- a/solution.py
+++ b/solution.py
@@ -89,7 +89,9 @@
     keys_part = lax.all_gather(keys, "patch", axis=0, tiled=True)
     values_part = lax.all_gather(values, "patch", axis=0, tiled=True)
     sizes_part = lax.all_gather(sizes, "patch", axis=0, tiled=True)
-    alive_part = lax.all_gather(alive, "patch", axis=0, tiled=True)
+    alive_part = jnp.concatenate(
+        lax.all_to_all(jnp.stack([alive] * lax.axis_size("patch")), "patch", 0, 0), axis=0
+    )
     bias = jnp.where(alive_part > 0, size_bias(sizes_part), -1e30)
     top, total, accum = attend_piece(
         query_heads, empty_carry(heads, rows, head_size), keys_part, values_part, bias, inverse

time: 206 us -> 206 us (level)
  blocking collectives: 79 us -> 41.2 us
  waiting for transfers between devices: 63.3 us -> 92.1 us
  starting transfers between devices: 0.04 us -> 8.38 us
    all_gather x1 -> x0, blocking collectives: 36.4 us -> none  [body(): alive_part = lax.all_gather(alive, 'patch', axis=0, tiled=True)]
    all_gather x1, waiting for transfers between devices: 1.98 us -> 30.8 us  [body(): keys_part = lax.all_gather(keys, 'patch', axis=0, tiled=True)]
    all_to_all x0 -> x1, starting transfers between devices: none -> 8.34 us  [body(): lax.all_to_all(jnp.stack([alive] * lax.axis_size('patch')), 'patch', 0, 0)]
  transfers between devices with their start and end apart: 2 -> 3, of which waited for: 2 -> 2; matrix products, arithmetic and copies ran while one was open for 7% -> 8% of each run, Pallas kernels for 0% -> 0%
where the time goes in v1:
time: 206 us
  waiting for transfers between devices  92.1 us (45%)
  blocking collectives  41.2 us (20%)
  matrix products  23.3 us (11%)
  local copies, waits for them, and re-layouts  20.9 us (10%)
  between operations  14.2 us (7%)
  starting transfers between devices  8.38 us (4%)
  other arithmetic  5.63 us (3%)
    all_gather x1, waiting for transfers between devices, body(): values_part = lax.all_gather(values, 'patch', axis=0, tiled=True)  60.5 us
    all_gather x1, blocking collectives, body(): sizes_part = lax.all_gather(sizes, 'patch', axis=0, tiled=True)  41.2 us
    all_gather x1, waiting for transfers between devices, body(): keys_part = lax.all_gather(keys, 'patch', axis=0, tiled=True)  30.8 us
    dot_general x1, matrix products, attend_piece(): jnp.einsum('hqk,khe->hqe', probs.astype(jnp.bfloat16), value_heads, prefe...  10.9 us
    all_to_all x1, starting transfers between devices, body(): lax.all_to_all(jnp.stack([alive] * lax.axis_size('patch')), 'patch', 0, 0)  8.34 us
    all_gather x1, local copies, waits for them, and re-layouts, body(): keys_part = lax.all_gather(keys, 'patch', axis=0, tiled=True)  6.73 us
    all_gather x1, local copies, waits for them, and re-layouts, body(): values_part = lax.all_gather(values, 'patch', axis=0, tiled=True)  6.72 us
    unnamed x10, local copies, waits for them, and re-layouts  5.73 us
  transfers between devices with their start and end apart: 3, of which 2 were waited for; matrix products, arithmetic and copies ran while one was open for 8% of the time, Pallas kernels for 0%

profile of v1, /device:TPU:0, one launch (start us, length us, event | category | flops | bytes accessed | tf_op | source)
XLA Modules:
  0.0 205.6 jit_solution(15018438547929240242)
XLA Ops:
  6.5 0.0 copy-start
  6.5 0.0 all-gather.4.cloned.1.call-start
  6.5 0.9 convert_reduce_fusion
  7.5 1.4 fusion.26
  8.9 0.2 multiply_reduce_fusion
  9.1 0.7 broadcast_add_fusion
  9.8 4.7 %convolution_convert_fusion = bf16[128,3456]{1,0:T(8,128)(2,1)S(1)} fusion(bf16[1152,3456]{1,0:T(8,128)(2,1)} %param.14, f32[128,1152]{1,0:T(8,128)S(1)} %get-tuple-element.11, f32[1152]{0:T(1024)} %param.11, f32[1152]{0:T(1024)S(1)} %broadcast_add_fusion, f32[128]{0:T(128)S(1)} %add_rsqrt_fusion, f32[128]{0:T(128)S(1)} %broadcast_multiply_fusion), kind=kOutput, calls=%fused_computation.6 | convolution fusion | flops 1020395520 | bytes 9447424 | tf_op jit(solution)/shard_map/dot_general | solution.py:79
  14.5 0.9 fusion.25
  15.4 0.0 all-gather.4.cloned.1.call-update
  15.5 0.0 all-gather.6.cloned.1.call-start
  15.5 0.7 all-gather.6.cloned.1.call-update
  16.9 0.6 stack.2
  17.5 8.3 %all-to-all-start = ((bf16[16,1,128]{2,1,0:T(2,128)(2,1)}), bf16[16,1,128]{2,1,0:T(2,128)(2,1)S(1)}, u32[]{:S(2)}, u32[]{:S(2)}) async-start(bf16[16,1,128]{2,1,0:T(2,128)(2,1)} %stack.2), calls=%async_computation | async-start | bytes 16384 | tf_op jit(solution)/shard_map/all_to_all | solution.py:93
  25.8 0.2 copy.18
  26.0 41.2 %all-gather = bf16[16,1,128]{2,1,0:T(2,128)(2,1)S(1)} all-gather(bf16[1,1,128]{2,1,0:T(2,128)(2,1)S(1)} %get-tuple-element.8), channel_id=1, replica_groups=mesh['patch'=16,'batch'=2] {'patch'}, dimensions={0}, use_global_device_ids=true | all-gather | bytes 4352 | tf_op jit(solution)/shard_map/all_gather | solution.py:91
  67.2 0.0 all-to-all-done
  67.3 30.8 %all-gather.4.cloned.1.call-done = bf16[2048,1152]{1,0:T(8,128)(2,1)} async-done(((bf16[128,1152]{1,0:T(8,128)(2,1)}), bf16[2048,1152]{1,0:T(8,128)(2,1)}) %all-gather.4.cloned.1.call-update) | async-done | bytes 4718608 | tf_op jit(solution)/shard_map/all_gather | solution.py:89
  98.1 6.7 %copy.19 = bf16[2048,1152]{0,1:T(8,128)(2,1)} copy(bf16[2048,1152]{1,0:T(8,128)(2,1)} %all-gather.4.cloned.1.call-done) | data formatting | bytes 9437184 | tf_op jit(solution)/shard_map/all_gather | solution.py:89
  104.8 4.5 %fusion = (f32[16,128]{1,0:T(8,128)S(1)}, f32[16,128,2048]{2,1,0:T(8,128)S(1)}) fusion(f32[2048]{0:T(1024)S(1)} %bitcast.28, bf16[128,16,72]{0,2,1:T(8,128)(2,1)S(1)} %bitcast.26, bf16[2048,16,72]{0,2,1:T(8,128)(2,1)} %bitcast.24), kind=kOutput, calls=%fused_computation.2 | convolution fusion | flops 616560640 | bytes 21807104 | tf_op jit(solution)/shard_map/qhe,khe->hqk/dot_general | solution.py:48
  109.3 0.0 copy-start.1
  109.3 5.7 %copy-done.1 = f32[16,128,2048]{2,1,0:T(8,128)} copy-done((f32[16,128,2048]{2,1,0:T(8,128)}, f32[16,128,2048]{2,1,0:T(8,128)S(1)}, u32[]{:S(2)}) %copy-start.1) | copy-done | bytes 16777240
  115.0 3.8 %fusion.1 = f32[16,128]{1,0:T(8,128)S(1)} fusion(f32[16,128,2048]{2,1,0:T(8,128)S(1)} %get-tuple-element.13, f32[16,128]{1,0:T(8,128)S(1)} %broadcast_maximum_fusion, f32[2048]{0:T(1024)S(1)} %bitcast.29), kind=kLoop, calls=%fused_computation.3 | loop fusion | flops 16775168 | bytes 16801792 | tf_op jit(solution)/shard_map/reduce_sum | solution.py:53
  118.8 60.5 %all-gather.6.cloned.1.call-done = bf16[2048,1152]{1,0:T(8,128)(2,1)} async-done(((bf16[128,1152]{1,0:T(8,128)(2,1)}), bf16[2048,1152]{1,0:T(8,128)(2,1)}) %all-gather.6.cloned.1.call-update) | async-done | bytes 4718608 | tf_op jit(solution)/shard_map/all_gather | solution.py:90
  179.4 6.7 %copy.20 = bf16[2048,1152]{0,1:T(8,128)(2,1)} copy(bf16[2048,1152]{1,0:T(8,128)(2,1)} %all-gather.6.cloned.1.call-done) | data formatting | bytes 9437184 | tf_op jit(solution)/shard_map/all_gather | solution.py:90
  186.1 0.0 copy-start.2
  186.1 10.9 %fusion.15 = bf16[128,16,72]{0,2,1:T(8,128)(2,1)S(1)} fusion(bf16[2048,16,72]{0,2,1:T(8,128)(2,1)} %bitcast.25, f32[16,128,2048]{2,1,0:T(8,128)} %copy-done.1, f32[16,128]{1,0:T(8,128)S(1)} %broadcast_maximum_fusion, f32[2048]{0:T(1024)S(1)} %bitcast.30, f32[128,16]{0,1:T(8,128)S(1)} %bitcast.31), kind=kOutput, calls=%fused_computation.15 | convolution fusion | flops 621051904 | bytes 21815296 | tf_op jit(solution)/shard_map/hqk,khe->hqe/dot_general | solution.py:54
  196.9 0.0 copy-done
  197.0 0.6 fusion.27
  197.6 0.0 copy-done.2
  197.6 0.0 copy-done.3
  197.6 0.0 copy-done.4
  197.6 1.2 fusion.8
  (8 shorter events, 0.1 us)
Async XLA Ops:
  6.5 190.4 %copy-start = (bf16[1152,1152]{1,0:T(8,128)(2,1)S(1)}, bf16[1152,1152]{1,0:T(8,128)(2,1)}, u32[]{:S(2)}) copy-start(bf16[1152,1152]{1,0:T(8,128)(2,1)} %param.15) | copy-start | bytes 7962628
  6.5 91.6 %all-gather.4.cloned.1.call-start = ((), (), s32[]{:S(2)}) async-start(), calls=%async_computation.1 | async-start | bytes 5013504 | tf_op jit(solution)/shard_map/all_gather | solution.py:89
  15.5 163.9 %all-gather.6.cloned.1.call-start = ((), (), s32[]{:S(2)}) async-start(), calls=%async_computation.2 | async-start | bytes 5013504 | tf_op jit(solution)/shard_map/all_gather | solution.py:90
  17.5 49.8 %all-to-all-start = ((bf16[16,1,128]{2,1,0:T(2,128)(2,1)}), bf16[16,1,128]{2,1,0:T(2,128)(2,1)S(1)}, u32[]{:S(2)}, u32[]{:S(2)}) async-start(bf16[16,1,128]{2,1,0:T(2,128)(2,1)} %stack.2), calls=%async_computation | async-start | bytes 16384 | tf_op jit(solution)/shard_map/all_to_all | solution.py:93
  109.3 5.7 %copy-start.1 = (f32[16,128,2048]{2,1,0:T(8,128)}, f32[16,128,2048]{2,1,0:T(8,128)S(1)}, u32[]{:S(2)}) copy-start(f32[16,128,2048]{2,1,0:T(8,128)S(1)} %get-tuple-element.13) | copy-start | bytes 50331652
  186.1 11.5 %copy-start.2 = (bf16[128,1152]{1,0:T(8,128)(2,1)S(1)}, bf16[128,1152]{1,0:T(8,128)(2,1)}, u32[]{:S(2)}) copy-start(bf16[128,1152]{1,0:T(8,128)(2,1)} %param.8) | copy-start | bytes 884740
  186.1 11.5 %copy-start.3 = (f32[1152]{0:T(1024)S(1)}, f32[1152]{0:T(1024)}, u32[]{:S(2)}) copy-start(f32[1152]{0:T(1024)} %param.13) | copy-start | bytes 13828
  186.1 11.5 %copy-start.4 = (s32[128]{0:T(128)S(1)}, s32[128]{0:T(128)}, u32[]{:S(2)}) copy-start(s32[128]{0:T(128)} %param.9) | copy-start | bytes 1540
Sparse Core Ops, SparseCore 0:
  15.6 82.4 all-gather.3
  100.9 78.4 all-gather.5
